TPU v7x, 32 devices: a whole 2x2x4 slice. The times are simulated.
32 devices in a mesh: seq: 2 (over y), fsdp: 16 (over z, x, core).
Axes of the slice: x: 2, y: 2, z: 4, core: 2. Of those that a mesh axis runs over, the one named last changes fastest.
Arguments:
- tokens: bfloat16 [16, 1024, 1024], P('fsdp', 'seq'), may hold values from -6 to 6
- grad_out: bfloat16 [16, 1024, 1024], P('fsdp', 'seq'), may hold values from -6 to 6
- segments: int32 [16, 1024], P('fsdp'), may hold values from 0 to 1, as said below
- padding: int32 [16, 1024], P('fsdp'), may hold values from 0 to 1, as said below
- adapter_ids: int32 [16, 1], P('fsdp'), may hold values from 0 to 7
- norm1_gain: bfloat16 [1024], P('fsdp'), may hold values from 0.5 to 1.5
- norm1_bias: bfloat16 [1024], P('fsdp'), may hold values from -1.1953125 to 1.1953125
- w_qkv: bfloat16 [1024, 3072], P('fsdp'), may hold values from -0.1875 to 0.1875
- w_proj: bfloat16 [1024, 1024], P('fsdp'), may hold values from -3 to 3
- proj_bias: bfloat16 [1024], P('fsdp'), may hold values from -1.796875 to 1.796875
- norm2_gain: bfloat16 [1024], P('fsdp'), may hold values from 0.5 to 1.5
- norm2_bias: bfloat16 [1024], P('fsdp'), may hold values from -1.1953125 to 1.1953125
- w_fc1: bfloat16 [1024, 4096], P('fsdp'), may hold values from -0.1875 to 0.1875
- fc1_bias: bfloat16 [4096], P('fsdp'), may hold values from -3 to 3
- w_fc2: bfloat16 [4096, 1024], P('fsdp'), may hold values from -0.09375 to 0.09375
- fc2_bias: bfloat16 [1024], P('fsdp'), may hold values from -1.796875 to 1.796875
- qkv_down: bfloat16 [1024, 128], replicated, may hold values from -0.1875 to 0.1875
- qkv_up: bfloat16 [128, 3072], replicated, may hold values from -1.5 to 1.5
- proj_down: bfloat16 [1024, 128], replicated, may hold values from -3 to 3
- proj_up: bfloat16 [128, 1024], replicated, may hold values from -1.5 to 1.5
- fc1_down: bfloat16 [1024, 128], replicated, may hold values from -0.1875 to 0.1875
- fc1_up: bfloat16 [128, 4096], replicated, may hold values from -1.5 to 1.5
- fc2_down: bfloat16 [4096, 128], replicated, may hold values from -0.09375 to 0.09375
- fc2_up: bfloat16 [128, 1024], replicated, may hold values from -1.5 to 1.5
Outputs:
- output: bfloat16 [16, 1024, 1024], P('fsdp', 'seq')
- grad_tokens: float32 [16, 1024, 1024], P('fsdp', 'seq')
- grad_qkv_down: float32 [1024, 128], replicated
- grad_qkv_up: float32 [128, 3072], replicated
- grad_proj_down: float32 [1024, 128], replicated
- grad_proj_up: float32 [128, 1024], replicated
- grad_fc1_down: float32 [1024, 128], replicated
- grad_fc1_up: float32 [128, 4096], replicated
- grad_fc2_down: float32 [4096, 128], replicated
- grad_fc2_up: float32 [128, 1024], replicated
Inputs may be any that keep to these rules, and one draw needn't show every extreme that they name: `segments`: in each pack the tokens with padding 1 form 1 runs of exactly 577 tokens, in order; a token's segment number is the count of runs that begin at or before it, so run s has number s and padding takes the number of the run before it, or 0. `padding`: 1 exactly on the tokens of the runs. `adapter_ids`: entry s - 1 is the adapter of run s of the pack.
All inputs are finite; a program needn't handle non-finite values.
Results may differ from a plain program's by a relative error of at most 0.014.
The roundings to bfloat16 on the way count: a program that leaves them out, or rounds other values in their place, can miss the bound.
Values may be sent and summed in bfloat16 or wider, within the bound.
A program may use at most 192 MiB of HBM per device.

v0:
```python
from functools import partial
import jax
import jax.numpy as jnp
from jax import lax
from jax.sharding import PartitionSpec as P

HEAD_DIM = 64
IMG = 577
RANK = 16
QBLOCK = 512
norm_eps = 1e-06
masked_score = -1e30


def matmul(left_side, right_side):
    return jnp.dot(left_side, right_side, preferred_element_type=jnp.float32)


def matmul_nt(left_side, right_side):
    return jnp.einsum("tk,jk->tj", left_side, right_side, preferred_element_type=jnp.float32)


def matmul_tn(left_side, right_side):
    return jnp.einsum("ti,to->io", left_side, right_side, preferred_element_type=jnp.float32)


def layer_norm(values, norm_gain, norm_shift):
    centre = jnp.mean(values, axis=-1, keepdims=True)
    centred = values - centre
    spread = jnp.mean(centred * centred, axis=-1, keepdims=True)
    return centred * lax.rsqrt(spread + norm_eps) * norm_gain + norm_shift


def norm_backward(values, norm_gain, norm_shift, grad_in):

    def apply_norm(inputs):
        return layer_norm(inputs, norm_gain, norm_shift)

    unused, pullback = jax.vjp(apply_norm, values)
    return pullback(grad_in)[0]


def selection(seg_own, image_adapters, columns):
    images = jnp.arange(image_adapters.shape[0], dtype=jnp.int32)
    image_match = seg_own[:, None] - 1 == images[None, :]
    token_adapter = jnp.sum(jnp.where(image_match, image_adapters[None, :], 0), axis=1)
    present = jnp.any(image_match, axis=1)
    column = jnp.arange(columns, dtype=jnp.int32) // RANK
    chosen = (token_adapter[:, None] == column[None, :]) & present[:, None]
    return chosen.astype(jnp.float32)


def adapter_forward(inputs_b, weight, down_map, up_map, select):
    inner_term = (matmul(inputs_b, down_map) * select).astype(jnp.bfloat16)
    return (matmul(inputs_b, weight) + matmul(inner_term, up_map), inner_term)


def adapter_backward(inputs_b, inner_term, grad_in, weight, down_map, up_map, select):
    grad_up = matmul_tn(inner_term, grad_in)
    grad_inner = (matmul_nt(grad_in, up_map) * select).astype(jnp.bfloat16)
    grad_down = matmul_tn(inputs_b, grad_inner)
    grad_inputs = matmul_nt(grad_in, weight) + matmul_nt(grad_inner, down_map)
    return (grad_inputs, grad_down, grad_up)


def block_scores(query_block, key_heads, seg_block, seg_keys, keep_keys):
    score_scale = HEAD_DIM ** (-0.5)
    scores = (
        jnp.einsum("qhd,khd->hqk", query_block, key_heads, preferred_element_type=jnp.float32)
        * score_scale
    )
    allowed = (seg_block[:, None] == seg_keys[None, :]) & (keep_keys[None, :] == 1)
    return jnp.where(allowed[None, :, :], scores, masked_score)


def split_heads(head_rows):
    all_rows = head_rows.shape[0]
    local_heads = head_rows.shape[2] // HEAD_DIM
    query_heads = head_rows[:, 0].reshape(all_rows, local_heads, HEAD_DIM)
    key_heads = head_rows[:, 1].reshape(all_rows, local_heads, HEAD_DIM)
    value_heads = head_rows[:, 2].reshape(all_rows, local_heads, HEAD_DIM)
    return (query_heads, key_heads, value_heads)


def key_window(all_rows):
    return min(all_rows, (QBLOCK + 2 * IMG - 2 + 127) // 128 * 128)


def window_start(block_index, all_rows, window):
    first = block_index * QBLOCK - (IMG - 1)
    return jnp.clip(first, 0, all_rows - window)


def attention_forward(head_rows, seg_all, keep_all):
    all_rows = head_rows.shape[0]
    block_count = all_rows // QBLOCK
    window = key_window(all_rows)
    query_heads, key_heads, value_heads = split_heads(head_rows)
    local_heads = query_heads.shape[1]

    def one_block(block_parts):
        query_block, seg_block, keep_block, block_index = block_parts
        start = window_start(block_index, all_rows, window)
        keys_near = lax.dynamic_slice_in_dim(key_heads, start, window, 0)
        values_near = lax.dynamic_slice_in_dim(value_heads, start, window, 0)
        seg_near = lax.dynamic_slice_in_dim(seg_all, start, window, 0)
        keep_near = lax.dynamic_slice_in_dim(keep_all, start, window, 0)
        scores = block_scores(query_block, keys_near, seg_block, seg_near, keep_near)
        row_max = jnp.max(scores, axis=2, keepdims=True)
        weights = jnp.exp(scores - row_max)
        row_sum = jnp.sum(weights, axis=2, keepdims=True)
        probs_low = (weights / row_sum).astype(jnp.bfloat16)
        result = jnp.einsum(
            "hqk,khd->qhd", probs_low, values_near, preferred_element_type=jnp.float32
        )
        result = result * keep_block[:, None, None].astype(jnp.float32)
        return (result.astype(jnp.bfloat16), row_max, row_sum)

    block_ids = jnp.arange(block_count, dtype=jnp.int32)
    blocked = (
        query_heads.reshape(block_count, QBLOCK, local_heads, HEAD_DIM),
        seg_all.reshape(block_count, QBLOCK),
        keep_all.reshape(block_count, QBLOCK),
        block_ids,
    )
    results, block_max, block_sums = lax.map(one_block, blocked)
    return (results.reshape(all_rows, local_heads * HEAD_DIM), block_max, block_sums)


def attention_backward(head_rows, grad_rows, seg_all, keep_all, block_max, block_sums):
    all_rows = head_rows.shape[0]
    block_count = all_rows // QBLOCK
    window = key_window(all_rows)
    query_heads, key_heads, value_heads = split_heads(head_rows)
    local_heads = query_heads.shape[1]
    score_scale = HEAD_DIM ** (-0.5)

    def one_block(running, block_parts):
        grad_keys, grad_values = running
        query_block, seg_block, keep_block, grad_block, row_max, row_sum, block_index = block_parts
        start = window_start(block_index, all_rows, window)
        keys_near = lax.dynamic_slice_in_dim(key_heads, start, window, 0)
        values_near = lax.dynamic_slice_in_dim(value_heads, start, window, 0)
        seg_near = lax.dynamic_slice_in_dim(seg_all, start, window, 0)
        keep_near = lax.dynamic_slice_in_dim(keep_all, start, window, 0)
        scores = block_scores(query_block, keys_near, seg_block, seg_near, keep_near)
        probs = jnp.exp(scores - row_max) / row_sum
        grad_result = grad_block * keep_block[:, None, None].astype(jnp.bfloat16)
        values_term = jnp.einsum(
            "hqk,qhd->khd",
            probs.astype(jnp.bfloat16),
            grad_result,
            preferred_element_type=jnp.float32,
        )
        grad_probs = jnp.einsum(
            "qhd,khd->hqk", grad_result, values_near, preferred_element_type=jnp.float32
        )
        row_inner = jnp.sum(probs * grad_probs, axis=2, keepdims=True)
        grad_scores = (probs * (grad_probs - row_inner)).astype(jnp.bfloat16)
        grad_query = (
            jnp.einsum("hqk,khd->qhd", grad_scores, keys_near, preferred_element_type=jnp.float32)
            * score_scale
        )
        keys_term = (
            jnp.einsum("hqk,qhd->khd", grad_scores, query_block, preferred_element_type=jnp.float32)
            * score_scale
        )
        grad_keys = lax.dynamic_update_slice_in_dim(
            grad_keys, lax.dynamic_slice_in_dim(grad_keys, start, window, 0) + keys_term, start, 0
        )
        grad_values = lax.dynamic_update_slice_in_dim(
            grad_values,
            lax.dynamic_slice_in_dim(grad_values, start, window, 0) + values_term,
            start,
            0,
        )
        return ((grad_keys, grad_values), grad_query)

    zero_heads = jnp.zeros((all_rows, local_heads, HEAD_DIM), jnp.float32)
    block_ids = jnp.arange(block_count, dtype=jnp.int32)
    blocked = (
        query_heads.reshape(block_count, QBLOCK, local_heads, HEAD_DIM),
        seg_all.reshape(block_count, QBLOCK),
        keep_all.reshape(block_count, QBLOCK),
        grad_rows.reshape(block_count, QBLOCK, local_heads, HEAD_DIM),
        block_max,
        block_sums,
        block_ids,
    )
    (grad_keys, grad_values), grad_queries = lax.scan(one_block, (zero_heads, zero_heads), blocked)
    flat_width = local_heads * HEAD_DIM
    stacked = jnp.stack(
        [
            grad_queries.reshape(all_rows, flat_width),
            grad_keys.reshape(all_rows, flat_width),
            grad_values.reshape(all_rows, flat_width),
        ],
        axis=1,
    )
    return stacked.astype(jnp.bfloat16)


def per_device(
    tokens,
    grad_out,
    segments,
    padding,
    adapter_ids,
    norm1_gain,
    norm1_bias,
    w_qkv,
    w_proj,
    proj_bias,
    norm2_gain,
    norm2_bias,
    w_fc1,
    fc1_bias,
    w_fc2,
    fc2_bias,
    qkv_down,
    qkv_up,
    proj_down,
    proj_up,
    fc1_down,
    fc1_up,
    fc2_down,
    fc2_up,
):
    tok_rows = tokens.shape[1]
    feat_width = tokens.shape[2]
    inputs = tokens[0].astype(jnp.float32)
    seg_all = segments[0]
    keep_all = padding[0]
    offset = lax.axis_index("seq") * tok_rows
    seg_own = lax.dynamic_slice_in_dim(seg_all, offset, tok_rows)
    select = selection(seg_own, adapter_ids[0], qkv_down.shape[1])
    gain_one, shift_one, qkv_weight, proj_weight, proj_shift = (
        lax.all_gather(norm1_gain, "fsdp", axis=0, tiled=True),
        lax.all_gather(norm1_bias, "fsdp", axis=0, tiled=True),
        lax.all_gather(w_qkv, "fsdp", axis=0, tiled=True),
        lax.all_gather(w_proj, "fsdp", axis=0, tiled=True),
        lax.all_gather(proj_bias, "fsdp", axis=0, tiled=True),
    )
    gain_one = gain_one.astype(jnp.float32)
    shift_one = shift_one.astype(jnp.float32)
    normed_one = layer_norm(inputs, gain_one, shift_one).astype(jnp.bfloat16)
    qkv_main, inner_one = adapter_forward(normed_one, qkv_weight, qkv_down, qkv_up, select)
    qkv_low = qkv_main.astype(jnp.bfloat16).reshape(tok_rows, 3, feat_width)
    head_rows = lax.all_to_all(qkv_low, "seq", split_axis=2, concat_axis=0, tiled=True)
    attended_heads, block_max, block_sums = attention_forward(head_rows, seg_all, keep_all)
    attended = lax.all_to_all(attended_heads, "seq", split_axis=0, concat_axis=1, tiled=True)
    branch_one, inner_two = adapter_forward(attended, proj_weight, proj_down, proj_up, select)
    middle = inputs + (branch_one + proj_shift.astype(jnp.float32))
    gain_two, shift_two, fc1_weight, fc2_shift, fc2_weight, fc1_shift = (
        lax.all_gather(norm2_gain, "fsdp", axis=0, tiled=True),
        lax.all_gather(norm2_bias, "fsdp", axis=0, tiled=True),
        lax.all_gather(w_fc1, "fsdp", axis=0, tiled=True),
        lax.all_gather(fc2_bias, "fsdp", axis=0, tiled=True),
        lax.all_gather(w_fc2, "fsdp", axis=0, tiled=True),
        lax.all_gather(fc1_bias, "fsdp", axis=0, tiled=True),
    )
    gain_two = gain_two.astype(jnp.float32)
    shift_two = shift_two.astype(jnp.float32)
    normed_two = layer_norm(middle, gain_two, shift_two).astype(jnp.bfloat16)
    hidden_main, inner_three = adapter_forward(normed_two, fc1_weight, fc1_down, fc1_up, select)
    hidden = hidden_main + fc1_shift.astype(jnp.float32)
    active = jax.nn.gelu(hidden, approximate=False).astype(jnp.bfloat16)
    branch_two, inner_four = adapter_forward(active, fc2_weight, fc2_down, fc2_up, select)
    output = (middle + (branch_two + fc2_shift.astype(jnp.float32))).astype(jnp.bfloat16)
    fc1_back, fc2_back = (
        lax.all_gather(w_fc1, "fsdp", axis=0, tiled=True),
        lax.all_gather(w_fc2, "fsdp", axis=0, tiled=True),
    )
    grad_top = grad_out[0]
    grad_active, grad_fc2_down, grad_fc2_up = adapter_backward(
        active, inner_four, grad_top, fc2_back, fc2_down, fc2_up, select
    )
    unused, gelu_back = jax.vjp(partial(jax.nn.gelu, approximate=False), hidden)
    grad_hidden = gelu_back(grad_active)[0].astype(jnp.bfloat16)
    grad_normed_two, grad_fc1_down, grad_fc1_up = adapter_backward(
        normed_two, inner_three, grad_hidden, fc1_back, fc1_down, fc1_up, select
    )
    grad_middle = grad_top.astype(jnp.float32) + norm_backward(
        middle, gain_two, shift_two, grad_normed_two
    )
    qkv_back, proj_back = (
        lax.all_gather(w_qkv, "fsdp", axis=0, tiled=True),
        lax.all_gather(w_proj, "fsdp", axis=0, tiled=True),
    )
    grad_branch_one = grad_middle.astype(jnp.bfloat16)
    grad_attended, grad_proj_down, grad_proj_up = adapter_backward(
        attended, inner_two, grad_branch_one, proj_back, proj_down, proj_up, select
    )
    grad_head_rows = lax.all_to_all(
        grad_attended.astype(jnp.bfloat16), "seq", split_axis=1, concat_axis=0, tiled=True
    )
    grad_qkv_heads = attention_backward(
        head_rows, grad_head_rows, seg_all, keep_all, block_max, block_sums
    )
    grad_qkv = lax.all_to_all(
        grad_qkv_heads, "seq", split_axis=0, concat_axis=2, tiled=True
    ).reshape(tok_rows, 3 * feat_width)
    grad_normed_one, grad_qkv_down, grad_qkv_up = adapter_backward(
        normed_one, inner_one, grad_qkv, qkv_back, qkv_down, qkv_up, select
    )
    grad_tokens = grad_middle + norm_backward(inputs, gain_one, shift_one, grad_normed_one)
    summed = lax.psum(
        (
            grad_qkv_down,
            grad_qkv_up,
            grad_proj_down,
            grad_proj_up,
            grad_fc1_down,
            grad_fc1_up,
            grad_fc2_down,
            grad_fc2_up,
        ),
        ("seq", "fsdp"),
    )
    return (
        output[None],
        grad_tokens[None],
        summed[0],
        summed[1],
        summed[2],
        summed[3],
        summed[4],
        summed[5],
        summed[6],
        summed[7],
    )


def solution(mesh):
    return jax.shard_map(
        per_device,
        mesh=mesh,
        in_specs=(
            P("fsdp", "seq", None),
            P("fsdp", "seq", None),
            P("fsdp", None),
            P("fsdp", None),
            P("fsdp", None),
            P("fsdp"),
            P("fsdp"),
            P("fsdp", None),
            P("fsdp", None),
            P("fsdp"),
            P("fsdp"),
            P("fsdp"),
            P("fsdp", None),
            P("fsdp"),
            P("fsdp", None),
            P("fsdp"),
            P(),
            P(),
            P(),
            P(),
            P(),
            P(),
            P(),
            P(),
        ),
        out_specs=(
            P("fsdp", "seq", None),
            P("fsdp", "seq", None),
            P(),
            P(),
            P(),
            P(),
            P(),
            P(),
            P(),
            P(),
        ),
        check_vma=False,
    )
```

profile of v0, /device:TPU:0, one launch (start us, length us, event | category | flops | bytes accessed | tf_op | source)
XLA Modules:
  0.0 709.4 jit_solution(8467365100569532765)
XLA Ops:
  17.0 65.1 %all-reduce.7 = (bf16[1024]{0:T(1024)(128)(2,1)S(1)}, bf16[1024]{0:T(1024)(128)(2,1)S(1)}, bf16[1024]{0:T(1024)(128)(2,1)}, bf16[1024]{0:T(1024)(128)(2,1)}, bf1...) all-reduce(bf16[1024]{0:T(1024)(128)(2,1)S(1)} %dynamic-update-slice.1, ...), channel_id=1, replica_groups=mesh['seq'=2,'fsdp'=16] {'fsdp'}, use_global_device_ids=true, to_apply=%add.1 | all-reduce | flops 6144 | bytes 24576
  88.8 5.6 fusion.69
  101.7 6.6 copy.78
  108.4 5.7 all-to-all-start
  116.6 41.0 %all-to-all-done = bf16[512,3,1024]{0,1,2:T(4,128)(2,1)} async-done(((bf16[512,3,1024]{0,1,2:T(4,128)(2,1)}), bf16[512,3,1024]{0,1,2:T(4,128)(2,1)}, u32[]{:S(2)}, u32[]{:S(2)}) %all-to-all-start) | async-done | bytes 3145760 | tf_op jit(solution)/shard_map/all_to_all | solution.py:249
  157.6 4.7 copy.79
  162.3 4.8 copy.80
  179.7 30.4 %while.31 = (s32[]{:T(128)}, bf16[2,512,8,64]{1,3,2,0:T(8,128)(2,1)}, f32[2,8,512,1]{2,1,3,0:T(8,128)S(1)}, f32[2,8,512,1]{2,1,3,0:T(8,128)S(1)}, s32[2,512]{1,0...) while((s32[]{:T(128)}, ...), condition=%wide.region_5.6_spmd, body=%wide.region_2.5_spmd.sunk | while | flops 1125639680 | bytes 64133320 | solution.py:126
  188.5 5.4 fusion.169
  203.7 5.4 fusion.169
  215.2 18.0 %all-gather = bf16[16,1,256]{2,1,0:T(2,128)(2,1)S(1)} all-gather(bf16[1,1,256]{2,1,0:T(2,128)(2,1)S(1)} %reshape.288), channel_id=1, replica_groups=mesh['seq'=2,'fsdp'=16] {'fsdp'}, dimensions={0}, use_global_device_ids=true | all-gather | bytes 8704 | tf_op jit(solution)/shard_map/all_gather | solution.py:260
  245.5 7.7 %fusion.71 = f32[512,4096]{1,0:T(8,128)S(1)} fusion(bf16[512,1024]{1,0:T(8,128)(2,1)} %copy-done.26, bf16[1024,4096]{1,0:T(8,128)(2,1)} %all-gather.10.cloned.1.call-done), kind=kOutput, calls=%fused_computation.141 | convolution fusion | flops 4294967296 | bytes 17825792 | tf_op jit(solution)/shard_map/dot_general | solution.py:16
  253.2 21.1 %multiply_convert_fusion.1 = (bf16[512,4096]{1,0:T(8,128)(2,1)}, f32[512,4096]{1,0:T(8,128)}, f32[512,4096]{1,0:T(8,128)}) fusion(f32[4096]{0:T(1024)S(1)} %bitcast.250, f32[512,4096]{1,0:T(8,128)S(1)} %fusion.71, bf16[512,128]{1,0:T(8,128)(2,1)S(1)} %fusion.51, bf16[128,4096]{1,0:T(8,128)(2,1)S(1)} %copy-done), kind=kOutput, calls=%fused_computation.53 | convolution fusion | flops 677380096 | bytes 30556160 | tf_op jit(solution)/shard_map/dot_general | solution.py:16
  274.3 11.7 %fusion.60 = f32[512,4096]{1,0:T(8,128)} fusion(bf16[4096,1024]{1,0:T(8,128)(2,1)} %all-gather.12.cloned.1.call-done, bf16[1,512,1024]{2,1,0:T(8,128)(2,1)} %param.29), kind=kOutput, calls=%fused_computation.116 | convolution fusion | flops 4294967296 | bytes 17825792 | tf_op jit(solution)/shard_map/tk,jk->tj/dot_general | solution.py:20
  286.0 10.6 %add_convert_fusion = bf16[512,4096]{1,0:T(8,128)(2,1)S(1)} fusion(f32[512,4096]{1,0:T(8,128)} %get-tuple-element.444, f32[512,4096]{1,0:T(8,128)} %fusion.60, f32[512,4096]{1,0:T(8,128)} %get-tuple-element.458, bf16[512,128]{1,0:T(8,128)(2,1)S(1)} %copy-done.59, bf16[4096,128]{1,0:T(8,128)(2,1)S(1)} %copy-done.82), kind=kOutput, calls=%fused_computation.52 | convolution fusion | flops 568328192 | bytes 30539776 | tf_op jit(solution)/shard_map/tk,jk->tj/dot_general | solution.py:20
  319.9 9.6 %all-to-all-done.2 = bf16[512,2,512]{2,0,1:T(8,128)(2,1)} async-done(((bf16[512,2,512]{2,0,1:T(8,128)(2,1)}), bf16[512,2,512]{2,0,1:T(8,128)(2,1)}, u32[]{:S(2)}, u32[]{:S(2)}) %all-to-all-start.2) | async-done | bytes 1048608 | tf_op jit(solution)/shard_map/all_to_all | solution.py:294
  332.0 97.7 %while.32 = (s32[]{:T(128)}, f32[1024,8,64]{0,2,1:T(8,128)S(1)}, f32[1024,8,64]{0,2,1:T(8,128)}, bf16[2,512,8,64]{1,3,2,0:T(8,128)(2,1)}, bf16[2,512,8,64]{1,3,2...) while((s32[]{:T(128)}, f32[1024,8,64]{0,2,1:T(8,128)S(1)}, ...), condition=%wide.region_12.13_spmd.clone, body=%wide.region_10.12_spmd.clone.sunk | while | flops 2730751488 | bytes 175265136 | solution.py:190
  332.4 9.7 %fusion.177 = f32[8,512,1024]{2,1,0:T(8,128)} fusion(bf16[1024,8,64]{0,2,1:T(8,128)(2,1)} %get-tuple-element.712, bf16[2,512,8,64]{1,3,2,0:T(8,128)(2,1)} %get-tuple-element.710, s32[]{:T(128)S(6)} %copy.123, bf16[512]{0:T(512)(128)(2,1)S(1)} %convert_reduce_fusion.3), kind=kOutput, calls=%fused_computation.38.clone.1 | convolution fusion | flops 537133056 | bytes 18351108 | tf_op jit(solution)/shard_map/while/body/eval_jaxpr/qhd,khd->hqk/dot_general | solution.py:155
  342.1 14.8 %multiply_reduce_fusion.4 = (f32[8,512]{1,0:T(8,128)S(1)}, f32[8,512,1024]{2,1,0:T(8,128)}) fusion(f32[8,512,1024]{2,1,0:T(8,128)} %fusion.177, f32[8,512]{1,0:T(8,128)S(1)} %get-tuple-element.627, f32[8,512]{1,0:T(8,128)S(1)} %get-tuple-element.628, bf16[1024,8,64]{0,2,1:T(8,128)(2,1)S(1)} %get-tuple-element.707, ...), kind=kOutput, calls=%fused_computation.23.clone.1 | convolution fusion | flops 562032640 | bytes 35700740 | tf_op jit(solution)/shard_map/while/body/eval_jaxpr/qhd,khd->hqk/dot_general | solution.py:69
  357.0 11.5 %multiply_convert_fusion.3 = bf16[8,512,1024]{2,1,0:T(8,128)(2,1)S(1)} fusion(f32[8,512,1024]{2,1,0:T(8,128)} %get-tuple-element.629, f32[8,512,1024]{2,1,0:T(8,128)} %fusion.177, f32[8,512]{1,0:T(8,128)S(1)} %get-tuple-element.630), kind=kLoop, calls=%fused_computation.22.clone.1 | loop fusion | flops 12582912 | bytes 41959424 | tf_op jit(solution)/shard_map/while/body/eval_jaxpr/convert_element_type | solution.py:159
  368.5 7.8 %bitcast_add_fusion.5 = f32[1024,8,64]{0,2,1:T(8,128)S(1)} fusion(f32[1024,8,64]{0,2,1:T(8,128)S(1)} %copy-done.8, f32[8,512,1024]{2,1,0:T(8,128)} %get-tuple-element.629, pred[]{:T(512)S(6)} %compare.7, bf16[2,512,8,64]{1,3,2,0:T(8,128)(2,1)S(1)} %copy-done.13, s32[]{:T(128)S(6)} %copy.123, bf16[512]{0:T(512)(128)(2,1)S(1)} %convert_reduce_fusion.3), kind=kOutput, calls=%fused_computation.27.clone.1 | convolution fusion | flops 542375936 | bytes 21496836 | tf_op jit(solution)/shard_map/while/body/eval_jaxpr/hqk,qhd->khd/dot_general | solution.py:149
  381.3 9.7 %fusion.177 = f32[8,512,1024]{2,1,0:T(8,128)} fusion(bf16[1024,8,64]{0,2,1:T(8,128)(2,1)} %get-tuple-element.712, bf16[2,512,8,64]{1,3,2,0:T(8,128)(2,1)} %get-tuple-element.710, s32[]{:T(128)S(6)} %copy.123, bf16[512]{0:T(512)(128)(2,1)S(1)} %convert_reduce_fusion.3), kind=kOutput, calls=%fused_computation.38.clone.1 | convolution fusion | flops 537133056 | bytes 18351108 | tf_op jit(solution)/shard_map/while/body/eval_jaxpr/qhd,khd->hqk/dot_general | solution.py:155
  391.0 14.8 %multiply_reduce_fusion.4 = (f32[8,512]{1,0:T(8,128)S(1)}, f32[8,512,1024]{2,1,0:T(8,128)}) fusion(f32[8,512,1024]{2,1,0:T(8,128)} %fusion.177, f32[8,512]{1,0:T(8,128)S(1)} %get-tuple-element.627, f32[8,512]{1,0:T(8,128)S(1)} %get-tuple-element.628, bf16[1024,8,64]{0,2,1:T(8,128)(2,1)S(1)} %get-tuple-element.707, ...), kind=kOutput, calls=%fused_computation.23.clone.1 | convolution fusion | flops 562032640 | bytes 35700740 | tf_op jit(solution)/shard_map/while/body/eval_jaxpr/qhd,khd->hqk/dot_general | solution.py:69
  405.8 11.5 %multiply_convert_fusion.3 = bf16[8,512,1024]{2,1,0:T(8,128)(2,1)S(1)} fusion(f32[8,512,1024]{2,1,0:T(8,128)} %get-tuple-element.629, f32[8,512,1024]{2,1,0:T(8,128)} %fusion.177, f32[8,512]{1,0:T(8,128)S(1)} %get-tuple-element.630), kind=kLoop, calls=%fused_computation.22.clone.1 | loop fusion | flops 12582912 | bytes 41959424 | tf_op jit(solution)/shard_map/while/body/eval_jaxpr/convert_element_type | solution.py:159
  417.3 7.8 %bitcast_add_fusion.5 = f32[1024,8,64]{0,2,1:T(8,128)S(1)} fusion(f32[1024,8,64]{0,2,1:T(8,128)S(1)} %copy-done.8, f32[8,512,1024]{2,1,0:T(8,128)} %get-tuple-element.629, pred[]{:T(512)S(6)} %compare.7, bf16[2,512,8,64]{1,3,2,0:T(8,128)(2,1)S(1)} %copy-done.13, s32[]{:T(128)S(6)} %copy.123, bf16[512]{0:T(512)(128)(2,1)S(1)} %convert_reduce_fusion.3), kind=kOutput, calls=%fused_computation.27.clone.1 | convolution fusion | flops 542375936 | bytes 21496836 | tf_op jit(solution)/shard_map/while/body/eval_jaxpr/hqk,qhd->khd/dot_general | solution.py:149
  437.4 7.8 %copy.89 = bf16[1024,3,512]{2,1,0:T(4,128)(2,1)} copy(bf16[1024,3,512]{0,2,1:T(8,128)(2,1)} %pad_maximum_fusion) | data formatting | bytes 6291456 | tf_op jit(solution)/shard_map/stack | solution.py:192
  445.3 5.7 all-to-all-start.3
  462.5 35.9 %all-to-all-done.3 = bf16[1024,3,512]{2,1,0:T(4,128)(2,1)} async-done(((bf16[1024,3,512]{2,1,0:T(4,128)(2,1)}), bf16[1024,3,512]{2,1,0:T(4,128)(2,1)}, u32[]{:S(2)}, u32[]{:S(2)}) %all-to-all-start.3) | async-done | bytes 3145760 | tf_op jit(solution)/shard_map/all_to_all | solution.py:300
  503.0 4.8 copy.91
  514.5 8.4 %fusion.72 = f32[512,1024]{1,0:T(8,128)S(1)} fusion(bf16[512,4096]{1,0:T(8,128)(2,1)} %get-tuple-element.443, bf16[4096,1024]{1,0:T(8,128)(2,1)} %all-gather.12.cloned.1.call-done), kind=kOutput, calls=%fused_computation.142 | convolution fusion | flops 4294967296 | bytes 14680064 | tf_op jit(solution)/shard_map/dot_general | solution.py:16
  525.3 5.8 fusion.75
  535.0 156.9 %all-reduce.10.cloned.1.call-done = (f32[1024,128]{1,0:T(8,128)}, f32[128,3072]{1,0:T(8,128)}, f32[1024,128]{1,0:T(8,128)}, f32[128,1024]{1,0:T(8,128)}, f32[102...) async-done(((f32[1024,128]{1,0:T(8,128)}, f32[128,3072]{1,0:T(8,128)}, f32[1024,128]{1,0:T(8,128)}, f32[128,1024]{1,0:T(8,128)}, ...) | async-done | bytes 8388624 | tf_op jit(solution)/shard_map/psum | solution.py:307
  (339 shorter events, 156.6 us)
Async XLA Ops:
  7.2 246.0 %copy-start = (bf16[128,4096]{1,0:T(8,128)(2,1)S(1)}, bf16[128,4096]{1,0:T(8,128)(2,1)}, u32[]{:S(2)}) copy-start(bf16[128,4096]{1,0:T(8,128)(2,1)} %param.49) | copy-start | bytes 3145732
  7.2 81.1 %copy-start.55 = (bf16[1024,128]{1,0:T(8,128)(2,1)S(1)}, bf16[1024,128]{1,0:T(8,128)(2,1)}, u32[]{:S(2)}) copy-start(bf16[1024,128]{1,0:T(8,128)(2,1)} %param.44) | copy-start | bytes 786436
  7.2 81.6 %all-gather.6.cloned.1.call-start = ((), (), s32[]{:S(2)}) async-start(), calls=%async_computation.4 | async-start | bytes 6684672 | tf_op jit(solution)/shard_map/all_gather | solution.py:240
  7.9 229.5 %all-gather.8.cloned.1.call-start = ((), (), s32[]{:S(2)}) async-start(), calls=%async_computation.5 | async-start | bytes 2228224 | tf_op jit(solution)/shard_map/all_gather | solution.py:241
  8.7 236.8 %all-gather.10.cloned.1.call-start = ((), (), s32[]{:S(2)}) async-start(), calls=%async_computation.6 | async-start | bytes 8912896 | tf_op jit(solution)/shard_map/all_gather | solution.py:257
  108.4 49.2 %all-to-all-start = ((bf16[512,3,1024]{0,1,2:T(4,128)(2,1)}), bf16[512,3,1024]{0,1,2:T(4,128)(2,1)}, u32[]{:S(2)}, u32[]{:S(2)}) async-start(bf16[512,3,1024]{0,1,2:T(4,128)(2,1)} %copy.78), calls=%async_computation | async-start | bytes 8388608 | tf_op jit(solution)/shard_map/all_to_all | solution.py:249
  114.1 160.2 %all-gather.12.cloned.1.call-start = ((), (), s32[]{:S(2)}) async-start(), calls=%async_computation.7 | async-start | bytes 8912896 | tf_op jit(solution)/shard_map/all_gather | solution.py:259
  179.6 34.9 %copy-start.83 = (bf16[256]{0:T(256)(128)(2,1)S(1)}, bf16[256]{0:T(256)(128)(2,1)}, u32[]{:S(2)}) copy-start(bf16[256]{0:T(256)(128)(2,1)} %param.41) | copy-start | bytes 1540
  179.6 34.9 %copy-start.75 = (bf16[1024]{0:T(1024)(128)(2,1)S(1)}, bf16[1024]{0:T(1024)(128)(2,1)}, u32[]{:S(2)}) copy-start(bf16[1024]{0:T(1024)(128)(2,1)} %get-tuple-element.439) | copy-start | bytes 6148
  179.6 35.0 %copy-start.74 = (bf16[1024]{0:T(1024)(128)(2,1)S(1)}, bf16[1024]{0:T(1024)(128)(2,1)}, u32[]{:S(2)}) copy-start(bf16[1024]{0:T(1024)(128)(2,1)} %get-tuple-element.437) | copy-start | bytes 6148
  179.6 35.0 %copy-start.73 = (bf16[1024]{0:T(1024)(128)(2,1)S(1)}, bf16[1024]{0:T(1024)(128)(2,1)}, u32[]{:S(2)}) copy-start(bf16[1024]{0:T(1024)(128)(2,1)} %get-tuple-element.438) | copy-start | bytes 6148
  179.6 35.0 %copy-start.72 = (bf16[1024]{0:T(1024)(128)(2,1)S(1)}, bf16[1024]{0:T(1024)(128)(2,1)}, u32[]{:S(2)}) copy-start(bf16[1024]{0:T(1024)(128)(2,1)} %get-tuple-element.440) | copy-start | bytes 6148
  179.6 53.6 %copy-start.53 = (bf16[128,1024]{1,0:T(8,128)(2,1)S(1)}, bf16[128,1024]{1,0:T(8,128)(2,1)}, u32[]{:S(2)}) copy-start(bf16[128,1024]{1,0:T(8,128)(2,1)} %param.51) | copy-start | bytes 786436
  179.6 53.6 %copy-start.77 = (s32[512]{0:T(512)S(1)}, s32[512]{0:T(512)}, u32[]{:S(2)}) copy-start(s32[512]{0:T(512)} %copy-done.76) | copy-start | bytes 6148
  179.7 53.6 %copy-start.80 = (pred[512]{0:T(512)(128)(4,1)S(1)}, pred[512]{0:T(512)(128)(4,1)}, u32[]{:S(2)}) copy-start(pred[512]{0:T(512)(128)(4,1)} %copy-done.79) | copy-start | bytes 1540
  179.7 53.6 %copy-start.85 = (s32[128]{0:T(128)S(1)}, s32[128]{0:T(128)}, u32[]{:S(2)}) copy-start(s32[128]{0:T(128)} %copy-done.84) | copy-start | bytes 1540
  210.1 25.5 %all-to-all-start.1 = ((bf16[2,512,512]{1,2,0:T(8,128)(2,1)}), bf16[2,512,512]{1,2,0:T(8,128)(2,1)}, u32[]{:S(2)}, u32[]{:S(2)}) async-start(bf16[2,512,512]{1,2,0:T(8,128)(2,1)} %bitcast.244), calls=%async_computation.1 | async-start | bytes 2097152 | tf_op jit(solution)/shard_map/all_to_all | solution.py:251
  274.3 11.7 %copy-start.59 = (bf16[512,128]{1,0:T(8,128)(2,1)S(1)}, bf16[512,128]{1,0:T(8,128)(2,1)}, u32[]{:S(2)}) copy-start(bf16[512,128]{1,0:T(8,128)(2,1)} %fusion.53) | copy-start | bytes 393220
  274.3 11.7 %copy-start.82 = (bf16[4096,128]{1,0:T(8,128)(2,1)S(1)}, bf16[4096,128]{1,0:T(8,128)(2,1)}, u32[]{:S(2)}) copy-start(bf16[4096,128]{1,0:T(8,128)(2,1)} %param.50) | copy-start | bytes 3145732
  274.3 24.4 %slice-start = ((s8[8388608]{0:T(1024)(128)(4,1)}), s8[4194304]{0:T(1024)(128)(4,1)S(1)}, s32[]{:S(2)}) async-start(s8[8388608]{0:T(1024)(128)(4,1)} %bitcast.251), calls=%async_computation.9 | async-start | bytes 8388608
  286.0 12.7 %slice-start.1 = ((s8[8388608]{0:T(1024)(128)(4,1)}), s8[4194304]{0:T(1024)(128)(4,1)S(1)}, s32[]{:S(2)}) async-start(s8[8388608]{0:T(1024)(128)(4,1)} %bitcast.251), calls=%async_computation.10 | async-start | bytes 8388608
  310.4 21.5 %copy-start.3 = (bf16[1024,8,64]{0,2,1:T(8,128)(2,1)S(1)}, bf16[1024,8,64]{0,2,1:T(8,128)(2,1)}, u32[]{:S(2)}) copy-start(bf16[1024,8,64]{0,2,1:T(8,128)(2,1)} %copy-done.2) | copy-start | bytes 3145732
  310.4 19.1 %all-to-all-start.2 = ((bf16[512,2,512]{2,0,1:T(8,128)(2,1)}), bf16[512,2,512]{2,0,1:T(8,128)(2,1)}, u32[]{:S(2)}, u32[]{:S(2)}) async-start(bf16[512,2,512]{2,0,1:T(8,128)(2,1)} %bitcast.241), calls=%async_computation.2 | async-start | bytes 2097152 | tf_op jit(solution)/shard_map/all_to_all | solution.py:294
  332.4 9.7 %copy-start.14 = (bf16[2,512,8,64]{1,3,2,0:T(8,128)(2,1)S(1)}, bf16[2,512,8,64]{1,3,2,0:T(8,128)(2,1)}, u32[]{:S(2)}) copy-start(bf16[2,512,8,64]{1,3,2,0:T(8,128)(2,1)} %get-tuple-element.703) | copy-start | bytes 3145732 | tf_op jit(solution)/shard_map/while
  357.0 11.5 %copy-start.8 = (f32[1024,8,64]{0,2,1:T(8,128)S(1)}, f32[1024,8,64]{0,2,1:T(8,128)}, u32[]{:S(2)}) copy-start(f32[1024,8,64]{0,2,1:T(8,128)} %get-tuple-element.685) | copy-start | bytes 6291460 | tf_op jit(solution)/shard_map/while
  357.0 11.5 %copy-start.13 = (bf16[2,512,8,64]{1,3,2,0:T(8,128)(2,1)S(1)}, bf16[2,512,8,64]{1,3,2,0:T(8,128)(2,1)}, u32[]{:S(2)}) copy-start(bf16[2,512,8,64]{1,3,2,0:T(8,128)(2,1)} %get-tuple-element.710) | copy-start | bytes 3145732 | tf_op jit(solution)/shard_map/while
  381.3 9.7 %copy-start.14 = (bf16[2,512,8,64]{1,3,2,0:T(8,128)(2,1)S(1)}, bf16[2,512,8,64]{1,3,2,0:T(8,128)(2,1)}, u32[]{:S(2)}) copy-start(bf16[2,512,8,64]{1,3,2,0:T(8,128)(2,1)} %get-tuple-element.703) | copy-start | bytes 3145732 | tf_op jit(solution)/shard_map/while
  405.8 11.5 %copy-start.8 = (f32[1024,8,64]{0,2,1:T(8,128)S(1)}, f32[1024,8,64]{0,2,1:T(8,128)}, u32[]{:S(2)}) copy-start(f32[1024,8,64]{0,2,1:T(8,128)} %get-tuple-element.685) | copy-start | bytes 6291460 | tf_op jit(solution)/shard_map/while
  405.8 11.5 %copy-start.13 = (bf16[2,512,8,64]{1,3,2,0:T(8,128)(2,1)S(1)}, bf16[2,512,8,64]{1,3,2,0:T(8,128)(2,1)}, u32[]{:S(2)}) copy-start(bf16[2,512,8,64]{1,3,2,0:T(8,128)(2,1)} %get-tuple-element.710) | copy-start | bytes 3145732 | tf_op jit(solution)/shard_map/while
  445.3 53.1 %all-to-all-start.3 = ((bf16[1024,3,512]{2,1,0:T(4,128)(2,1)}), bf16[1024,3,512]{2,1,0:T(4,128)(2,1)}, u32[]{:S(2)}, u32[]{:S(2)}) async-start(bf16[1024,3,512]{2,1,0:T(4,128)(2,1)} %copy.89), calls=%async_computation.3 | async-start | bytes 8388608 | tf_op jit(solution)/shard_map/all_to_all | solution.py:300
  451.0 240.9 %all-reduce.10.cloned.1.call-start = ((), (), s32[]{:S(2)}) async-start(), calls=%async_computation.8 | async-start | bytes 16777216 | tf_op jit(solution)/shard_map/psum | solution.py:307
  514.5 8.4 %copy-start.7 = (f32[512,1024]{1,0:T(8,128)S(1)}, f32[512,1024]{1,0:T(8,128)}, u32[]{:S(2)}) copy-start(f32[512,1024]{1,0:T(8,128)} %copy-done.5) | copy-start | bytes 6291460
  (74 other events, 313.6 us)
Sparse Core Ops, SparseCore 0:
  10.3 64.6 all-gather.5
  77.2 40.2 all-gather.7
  119.6 73.0 all-gather.9
  194.7 72.8 all-gather.11
  514.6 177.2 all-reduce.9
where the time goes:
time: 718 us; the launch traced here: 709 us
  waiting for transfers between devices  246 us (34%)
  matrix products  210 us (29%)
  local copies, waits for them, and re-layouts  85.6 us (12%)
  blocking collectives  83.1 us (12%)
  other arithmetic  47.5 us (7%)
  starting transfers between devices  20.8 us (3%)
  between operations  16.7 us (2%)
    psum x1, waiting for transfers between devices, per_device(): lax.psum((grad_qkv_down, grad_qkv_up, grad_proj_down, grad_proj_up, grad_...  157 us
    unnamed x1, blocking collectives  65.1 us
    dot_general x12, matrix products, matmul(): return jnp.dot(left_side, right_side, preferred_element_type=jnp.float32)  58.6 us
    dot_general x12, matrix products, matmul_nt(): jnp.einsum('tk,jk->tj', left_side, right_side, preferred_element_type=jnp...  43 us
    all_to_all x1, waiting for transfers between devices, per_device(): lax.all_to_all(qkv_low, 'seq', split_axis=2, concat_axis=0, tiled=True)  41 us
    dot_general x4, matrix products, block_scores(): jnp.einsum('qhd,khd->hqk', query_block, key_heads, preferred_element_type...  37.9 us
    all_to_all x1, waiting for transfers between devices, per_device(): lax.all_to_all(grad_qkv_heads, 'seq', split_axis=0, concat_axis=2, tiled=...  35.9 us
    unnamed x185, local copies, waits for them, and re-layouts  25.5 us
  transfers between devices with their start and end apart: 9, of which 4 were waited for; matrix products, arithmetic and copies ran while one was open for 22% of the time, Pallas kernels for 0%

commit v1 on v0

--- a/solution.py
+++ b/solution.py
@@ -305,17 +305,20 @@
     )
     grad_tokens = grad_middle + norm_backward(inputs, gain_one, shift_one, grad_normed_one)
     summed = lax.psum(
-        (
-            grad_qkv_down,
-            grad_qkv_up,
-            grad_proj_down,
-            grad_proj_up,
-            grad_fc1_down,
-            grad_fc1_up,
-            grad_fc2_down,
-            grad_fc2_up,
+        lax.psum(
+            (
+                grad_qkv_down,
+                grad_qkv_up,
+                grad_proj_down,
+                grad_proj_up,
+                grad_fc1_down,
+                grad_fc1_up,
+                grad_fc2_down,
+                grad_fc2_up,
+            ),
+            "fsdp",
         ),
-        ("seq", "fsdp"),
+        "seq",
     )
     return (
         output[None],

time: 718 us -> 909 us (1.27)
  waiting for transfers between devices: 246 us -> 437 us
    psum x0 -> x1, waiting for transfers between devices: none -> 180 us  [per_device(): lax.psum(lax.psum((grad_qkv_down, grad_qkv_up, grad_proj_down, grad_proj_...]
    psum x1, waiting for transfers between devices: 157 us -> 168 us  [per_device(): lax.psum((grad_qkv_down, grad_qkv_up, grad_proj_down, grad_proj_up, grad_...]
    unnamed x185 -> x183, local copies, waits for them, and re-layouts: 25.5 us -> 26.1 us
  transfers between devices with their start and end apart: 9 -> 10, of which waited for: 4 -> 5; matrix products, arithmetic and copies ran while one was open for 22% -> 18% of each run, Pallas kernels for 0% -> 0%
where the time goes in v1:
time: 909 us; the launch traced here: 901 us
  waiting for transfers between devices  437 us (48%)
  matrix products  210 us (23%)
  local copies, waits for them, and re-layouts  86.1 us (9%)
  blocking collectives  83.2 us (9%)
  other arithmetic  46.8 us (5%)
  starting transfers between devices  20.8 us (2%)
  between operations  17 us (2%)
    psum x1, waiting for transfers between devices, per_device(): lax.psum(lax.psum((grad_qkv_down, grad_qkv_up, grad_proj_down, grad_proj_...  180 us
    psum x1, waiting for transfers between devices, per_device(): lax.psum((grad_qkv_down, grad_qkv_up, grad_proj_down, grad_proj_up, grad_...  168 us
    unnamed x1, blocking collectives  65.1 us
    dot_general x12, matrix products, matmul(): return jnp.dot(left_side, right_side, preferred_element_type=jnp.float32)  58.8 us
    dot_general x12, matrix products, matmul_nt(): jnp.einsum('tk,jk->tj', left_side, right_side, preferred_element_type=jnp...  42.9 us
    all_to_all x1, waiting for transfers between devices, per_device(): lax.all_to_all(qkv_low, 'seq', split_axis=2, concat_axis=0, tiled=True)  41 us
    dot_general x4, matrix products, block_scores(): jnp.einsum('qhd,khd->hqk', query_block, key_heads, preferred_element_type...  37.8 us
    all_to_all x1, waiting for transfers between devices, per_device(): lax.all_to_all(grad_qkv_heads, 'seq', split_axis=0, concat_axis=2, tiled=...  36 us
  transfers between devices with their start and end apart: 10, of which 5 were waited for; matrix products, arithmetic and copies ran while one was open for 18% of the time, Pallas kernels for 0%

profile of v1, /device:TPU:0, one launch (start us, length us, event | category | flops | bytes accessed | tf_op | source)
XLA Modules:
  0.0 900.8 jit_solution(5816522163426195007)
XLA Ops:
  17.0 65.1 %all-reduce.8 = (bf16[1024]{0:T(1024)(128)(2,1)S(1)}, bf16[1024]{0:T(1024)(128)(2,1)S(1)}, bf16[1024]{0:T(1024)(128)(2,1)}, bf16[1024]{0:T(1024)(128)(2,1)}, bf1...) all-reduce(bf16[1024]{0:T(1024)(128)(2,1)S(1)} %dynamic-update-slice.1, ...), channel_id=1, replica_groups=mesh['seq'=2,'fsdp'=16] {'fsdp'}, use_global_device_ids=true, to_apply=%add.1 | all-reduce | flops 6144 | bytes 24576
  88.8 5.6 fusion.69
  101.7 6.6 copy.78
  108.3 5.7 all-to-all-start
  116.6 41.0 %all-to-all-done = bf16[512,3,1024]{0,1,2:T(4,128)(2,1)} async-done(((bf16[512,3,1024]{0,1,2:T(4,128)(2,1)}), bf16[512,3,1024]{0,1,2:T(4,128)(2,1)}, u32[]{:S(2)}, u32[]{:S(2)}) %all-to-all-start) | async-done | bytes 3145760 | tf_op jit(solution)/shard_map/all_to_all | solution.py:249
  162.2 4.7 copy.80
  179.6 30.4 %while.31 = (s32[]{:T(128)}, bf16[2,512,8,64]{1,3,2,0:T(8,128)(2,1)}, f32[2,8,512,1]{2,1,3,0:T(8,128)S(1)}, f32[2,8,512,1]{2,1,3,0:T(8,128)S(1)}, s32[2,512]{1,0...) while((s32[]{:T(128)}, ...), condition=%wide.region_5.6_spmd, body=%wide.region_2.5_spmd.sunk | while | flops 1125639680 | bytes 64133320 | solution.py:126
  188.5 5.4 fusion.169
  203.6 5.4 fusion.169
  214.5 18.1 %all-gather = bf16[16,1,256]{2,1,0:T(2,128)(2,1)S(1)} all-gather(bf16[1,1,256]{2,1,0:T(2,128)(2,1)S(1)} %reshape.288), channel_id=1, replica_groups=mesh['seq'=2,'fsdp'=16] {'fsdp'}, dimensions={0}, use_global_device_ids=true | all-gather | bytes 8704 | tf_op jit(solution)/shard_map/all_gather | solution.py:260
  244.9 7.7 fusion.71
  252.7 21.2 %multiply_convert_fusion.1 = (bf16[512,4096]{1,0:T(8,128)(2,1)}, f32[512,4096]{1,0:T(8,128)}, f32[512,4096]{1,0:T(8,128)}) fusion(f32[4096]{0:T(1024)S(1)} %bitcast.250, f32[512,4096]{1,0:T(8,128)S(1)} %fusion.71, bf16[512,128]{1,0:T(8,128)(2,1)S(1)} %fusion.51, bf16[128,4096]{1,0:T(8,128)(2,1)S(1)} %copy-done), kind=kOutput, calls=%fused_computation.53 | convolution fusion | flops 677380096 | bytes 30556160 | tf_op jit(solution)/shard_map/dot_general | solution.py:16
  273.9 11.7 %fusion.60 = f32[512,4096]{1,0:T(8,128)} fusion(bf16[4096,1024]{1,0:T(8,128)(2,1)} %all-gather.12.cloned.1.call-done, bf16[1,512,1024]{2,1,0:T(8,128)(2,1)} %param.29), kind=kOutput, calls=%fused_computation.116 | convolution fusion | flops 4294967296 | bytes 17825792 | tf_op jit(solution)/shard_map/tk,jk->tj/dot_general | solution.py:20
  285.6 10.6 %add_convert_fusion = bf16[512,4096]{1,0:T(8,128)(2,1)S(1)} fusion(f32[512,4096]{1,0:T(8,128)} %get-tuple-element.452, f32[512,4096]{1,0:T(8,128)} %fusion.60, f32[512,4096]{1,0:T(8,128)} %get-tuple-element.466, bf16[512,128]{1,0:T(8,128)(2,1)S(1)} %copy-done.59, bf16[4096,128]{1,0:T(8,128)(2,1)S(1)} %copy-done.81), kind=kOutput, calls=%fused_computation.52 | convolution fusion | flops 568328192 | bytes 30539776 | tf_op jit(solution)/shard_map/tk,jk->tj/dot_general | solution.py:20
  319.5 9.7 %all-to-all-done.2 = bf16[512,2,512]{2,0,1:T(8,128)(2,1)} async-done(((bf16[512,2,512]{2,0,1:T(8,128)(2,1)}), bf16[512,2,512]{2,0,1:T(8,128)(2,1)}, u32[]{:S(2)}, u32[]{:S(2)}) %all-to-all-start.2) | async-done | bytes 1048608 | tf_op jit(solution)/shard_map/all_to_all | solution.py:294
  331.6 97.7 %while.32 = (s32[]{:T(128)}, f32[1024,8,64]{0,2,1:T(8,128)S(1)}, f32[1024,8,64]{0,2,1:T(8,128)}, bf16[2,512,8,64]{1,3,2,0:T(8,128)(2,1)}, bf16[2,512,8,64]{1,3,2...) while((s32[]{:T(128)}, f32[1024,8,64]{0,2,1:T(8,128)S(1)}, ...), condition=%wide.region_12.13_spmd.clone, body=%wide.region_10.12_spmd.clone.sunk | while | flops 2730751488 | bytes 175265136 | solution.py:190
  332.1 9.7 %fusion.177 = f32[8,512,1024]{2,1,0:T(8,128)} fusion(bf16[1024,8,64]{0,2,1:T(8,128)(2,1)} %get-tuple-element.720, bf16[2,512,8,64]{1,3,2,0:T(8,128)(2,1)} %get-tuple-element.718, s32[]{:T(128)S(6)} %copy.123, bf16[512]{0:T(512)(128)(2,1)S(1)} %convert_reduce_fusion.3), kind=kOutput, calls=%fused_computation.38.clone.1 | convolution fusion | flops 537133056 | bytes 18351108 | tf_op jit(solution)/shard_map/while/body/eval_jaxpr/qhd,khd->hqk/dot_general | solution.py:155
  341.8 14.8 %multiply_reduce_fusion.4 = (f32[8,512]{1,0:T(8,128)S(1)}, f32[8,512,1024]{2,1,0:T(8,128)}) fusion(f32[8,512,1024]{2,1,0:T(8,128)} %fusion.177, f32[8,512]{1,0:T(8,128)S(1)} %get-tuple-element.635, f32[8,512]{1,0:T(8,128)S(1)} %get-tuple-element.636, bf16[1024,8,64]{0,2,1:T(8,128)(2,1)S(1)} %get-tuple-element.715, ...), kind=kOutput, calls=%fused_computation.23.clone.1 | convolution fusion | flops 562032640 | bytes 35700740 | tf_op jit(solution)/shard_map/while/body/eval_jaxpr/qhd,khd->hqk/dot_general | solution.py:69
  356.6 11.5 %multiply_convert_fusion.3 = bf16[8,512,1024]{2,1,0:T(8,128)(2,1)S(1)} fusion(f32[8,512,1024]{2,1,0:T(8,128)} %get-tuple-element.637, f32[8,512,1024]{2,1,0:T(8,128)} %fusion.177, f32[8,512]{1,0:T(8,128)S(1)} %get-tuple-element.638), kind=kLoop, calls=%fused_computation.22.clone.1 | loop fusion | flops 12582912 | bytes 41959424 | tf_op jit(solution)/shard_map/while/body/eval_jaxpr/convert_element_type | solution.py:159
  368.1 7.8 bitcast_add_fusion.5
  381.0 9.7 %fusion.177 = f32[8,512,1024]{2,1,0:T(8,128)} fusion(bf16[1024,8,64]{0,2,1:T(8,128)(2,1)} %get-tuple-element.720, bf16[2,512,8,64]{1,3,2,0:T(8,128)(2,1)} %get-tuple-element.718, s32[]{:T(128)S(6)} %copy.123, bf16[512]{0:T(512)(128)(2,1)S(1)} %convert_reduce_fusion.3), kind=kOutput, calls=%fused_computation.38.clone.1 | convolution fusion | flops 537133056 | bytes 18351108 | tf_op jit(solution)/shard_map/while/body/eval_jaxpr/qhd,khd->hqk/dot_general | solution.py:155
  390.6 14.8 %multiply_reduce_fusion.4 = (f32[8,512]{1,0:T(8,128)S(1)}, f32[8,512,1024]{2,1,0:T(8,128)}) fusion(f32[8,512,1024]{2,1,0:T(8,128)} %fusion.177, f32[8,512]{1,0:T(8,128)S(1)} %get-tuple-element.635, f32[8,512]{1,0:T(8,128)S(1)} %get-tuple-element.636, bf16[1024,8,64]{0,2,1:T(8,128)(2,1)S(1)} %get-tuple-element.715, ...), kind=kOutput, calls=%fused_computation.23.clone.1 | convolution fusion | flops 562032640 | bytes 35700740 | tf_op jit(solution)/shard_map/while/body/eval_jaxpr/qhd,khd->hqk/dot_general | solution.py:69
  405.5 11.5 %multiply_convert_fusion.3 = bf16[8,512,1024]{2,1,0:T(8,128)(2,1)S(1)} fusion(f32[8,512,1024]{2,1,0:T(8,128)} %get-tuple-element.637, f32[8,512,1024]{2,1,0:T(8,128)} %fusion.177, f32[8,512]{1,0:T(8,128)S(1)} %get-tuple-element.638), kind=kLoop, calls=%fused_computation.22.clone.1 | loop fusion | flops 12582912 | bytes 41959424 | tf_op jit(solution)/shard_map/while/body/eval_jaxpr/convert_element_type | solution.py:159
  417.0 7.8 bitcast_add_fusion.5
  437.0 7.8 copy.89
  444.8 5.7 all-to-all-start.3
  462.1 36.0 %all-to-all-done.3 = bf16[1024,3,512]{2,1,0:T(4,128)(2,1)} async-done(((bf16[1024,3,512]{2,1,0:T(4,128)(2,1)}), bf16[1024,3,512]{2,1,0:T(4,128)(2,1)}, u32[]{:S(2)}, u32[]{:S(2)}) %all-to-all-start.3) | async-done | bytes 3145760 | tf_op jit(solution)/shard_map/all_to_all | solution.py:300
  502.7 4.8 copy.91
  514.3 167.8 %all-reduce.12.cloned.1.call-done = (f32[1024,128]{1,0:T(8,128)}, f32[128,3072]{1,0:T(8,128)}, f32[1024,128]{1,0:T(8,128)}, f32[128,1024]{1,0:T(8,128)}, f32[102...) async-done(((f32[1024,128]{1,0:T(8,128)}, f32[128,3072]{1,0:T(8,128)}, f32[1024,128]{1,0:T(8,128)}, f32[128,1024]{1,0:T(8,128)}, ...) | async-done | bytes 8388624 | tf_op jit(solution)/shard_map/psum | solution.py:308
  682.7 8.6 fusion.72
  693.6 5.7 fusion.75
  703.1 179.8 %all-reduce.14.cloned.1.call-done = (f32[1024,128]{1,0:T(8,128)}, f32[128,3072]{1,0:T(8,128)}, f32[1024,128]{1,0:T(8,128)}, f32[128,1024]{1,0:T(8,128)}, f32[102...) async-done(((f32[1024,128]{1,0:T(8,128)}, f32[128,3072]{1,0:T(8,128)}, f32[1024,128]{1,0:T(8,128)}, f32[128,1024]{1,0:T(8,128)}, ...) | async-done | bytes 8388624 | tf_op jit(solution)/shard_map/psum | solution.py:307
  (340 shorter events, 161.2 us)
Async XLA Ops:
  7.2 245.5 %copy-start = (bf16[128,4096]{1,0:T(8,128)(2,1)S(1)}, bf16[128,4096]{1,0:T(8,128)(2,1)}, u32[]{:S(2)}) copy-start(bf16[128,4096]{1,0:T(8,128)(2,1)} %param.49) | copy-start | bytes 3145732
  7.2 81.1 %copy-start.55 = (bf16[1024,128]{1,0:T(8,128)(2,1)S(1)}, bf16[1024,128]{1,0:T(8,128)(2,1)}, u32[]{:S(2)}) copy-start(bf16[1024,128]{1,0:T(8,128)(2,1)} %param.44) | copy-start | bytes 786436
  7.2 81.6 %all-gather.6.cloned.1.call-start = ((), (), s32[]{:S(2)}) async-start(), calls=%async_computation.4 | async-start | bytes 6684672 | tf_op jit(solution)/shard_map/all_gather | solution.py:240
  7.9 228.9 %all-gather.8.cloned.1.call-start = ((), (), s32[]{:S(2)}) async-start(), calls=%async_computation.5 | async-start | bytes 2228224 | tf_op jit(solution)/shard_map/all_gather | solution.py:241
  8.7 236.2 %all-gather.10.cloned.1.call-start = ((), (), s32[]{:S(2)}) async-start(), calls=%async_computation.6 | async-start | bytes 8912896 | tf_op jit(solution)/shard_map/all_gather | solution.py:257
  108.3 49.2 %all-to-all-start = ((bf16[512,3,1024]{0,1,2:T(4,128)(2,1)}), bf16[512,3,1024]{0,1,2:T(4,128)(2,1)}, u32[]{:S(2)}, u32[]{:S(2)}) async-start(bf16[512,3,1024]{0,1,2:T(4,128)(2,1)} %copy.78), calls=%async_computation | async-start | bytes 8388608 | tf_op jit(solution)/shard_map/all_to_all | solution.py:249
  114.1 159.8 %all-gather.12.cloned.1.call-start = ((), (), s32[]{:S(2)}) async-start(), calls=%async_computation.7 | async-start | bytes 8912896 | tf_op jit(solution)/shard_map/all_gather | solution.py:259
  179.6 34.9 %copy-start.82 = (bf16[256]{0:T(256)(128)(2,1)S(1)}, bf16[256]{0:T(256)(128)(2,1)}, u32[]{:S(2)}) copy-start(bf16[256]{0:T(256)(128)(2,1)} %param.41) | copy-start | bytes 1540
  179.6 34.9 %copy-start.74 = (bf16[1024]{0:T(1024)(128)(2,1)S(1)}, bf16[1024]{0:T(1024)(128)(2,1)}, u32[]{:S(2)}) copy-start(bf16[1024]{0:T(1024)(128)(2,1)} %get-tuple-element.447) | copy-start | bytes 6148
  179.6 34.9 %copy-start.73 = (bf16[1024]{0:T(1024)(128)(2,1)S(1)}, bf16[1024]{0:T(1024)(128)(2,1)}, u32[]{:S(2)}) copy-start(bf16[1024]{0:T(1024)(128)(2,1)} %get-tuple-element.445) | copy-start | bytes 6148
  179.6 34.9 %copy-start.72 = (bf16[1024]{0:T(1024)(128)(2,1)S(1)}, bf16[1024]{0:T(1024)(128)(2,1)}, u32[]{:S(2)}) copy-start(bf16[1024]{0:T(1024)(128)(2,1)} %get-tuple-element.446) | copy-start | bytes 6148
  179.6 53.1 %copy-start.53 = (bf16[128,1024]{1,0:T(8,128)(2,1)S(1)}, bf16[128,1024]{1,0:T(8,128)(2,1)}, u32[]{:S(2)}) copy-start(bf16[128,1024]{1,0:T(8,128)(2,1)} %param.51) | copy-start | bytes 786436
  179.6 53.1 %copy-start.76 = (s32[512]{0:T(512)S(1)}, s32[512]{0:T(512)}, u32[]{:S(2)}) copy-start(s32[512]{0:T(512)} %copy-done.75) | copy-start | bytes 6148
  179.6 53.1 %copy-start.79 = (pred[512]{0:T(512)(128)(4,1)S(1)}, pred[512]{0:T(512)(128)(4,1)}, u32[]{:S(2)}) copy-start(pred[512]{0:T(512)(128)(4,1)} %copy-done.78) | copy-start | bytes 1540
  179.6 53.1 %copy-start.84 = (s32[128]{0:T(128)S(1)}, s32[128]{0:T(128)}, u32[]{:S(2)}) copy-start(s32[128]{0:T(128)} %copy-done.83) | copy-start | bytes 1540
  210.0 25.0 %all-to-all-start.1 = ((bf16[2,512,512]{1,2,0:T(8,128)(2,1)}), bf16[2,512,512]{1,2,0:T(8,128)(2,1)}, u32[]{:S(2)}, u32[]{:S(2)}) async-start(bf16[2,512,512]{1,2,0:T(8,128)(2,1)} %bitcast.244), calls=%async_computation.1 | async-start | bytes 2097152 | tf_op jit(solution)/shard_map/all_to_all | solution.py:251
  273.8 11.7 %copy-start.59 = (bf16[512,128]{1,0:T(8,128)(2,1)S(1)}, bf16[512,128]{1,0:T(8,128)(2,1)}, u32[]{:S(2)}) copy-start(bf16[512,128]{1,0:T(8,128)(2,1)} %fusion.53) | copy-start | bytes 393220
  273.8 11.7 %copy-start.81 = (bf16[4096,128]{1,0:T(8,128)(2,1)S(1)}, bf16[4096,128]{1,0:T(8,128)(2,1)}, u32[]{:S(2)}) copy-start(bf16[4096,128]{1,0:T(8,128)(2,1)} %param.50) | copy-start | bytes 3145732
  273.8 24.4 %slice-start = ((s8[8388608]{0:T(1024)(128)(4,1)}), s8[4194304]{0:T(1024)(128)(4,1)S(1)}, s32[]{:S(2)}) async-start(s8[8388608]{0:T(1024)(128)(4,1)} %bitcast.251), calls=%async_computation.10 | async-start | bytes 8388608
  285.6 12.7 %slice-start.1 = ((s8[8388608]{0:T(1024)(128)(4,1)}), s8[4194304]{0:T(1024)(128)(4,1)S(1)}, s32[]{:S(2)}) async-start(s8[8388608]{0:T(1024)(128)(4,1)} %bitcast.251), calls=%async_computation.11 | async-start | bytes 8388608
  310.0 21.6 %copy-start.3 = (bf16[1024,8,64]{0,2,1:T(8,128)(2,1)S(1)}, bf16[1024,8,64]{0,2,1:T(8,128)(2,1)}, u32[]{:S(2)}) copy-start(bf16[1024,8,64]{0,2,1:T(8,128)(2,1)} %copy-done.2) | copy-start | bytes 3145732
  310.0 19.2 %all-to-all-start.2 = ((bf16[512,2,512]{2,0,1:T(8,128)(2,1)}), bf16[512,2,512]{2,0,1:T(8,128)(2,1)}, u32[]{:S(2)}, u32[]{:S(2)}) async-start(bf16[512,2,512]{2,0,1:T(8,128)(2,1)} %bitcast.241), calls=%async_computation.2 | async-start | bytes 2097152 | tf_op jit(solution)/shard_map/all_to_all | solution.py:294
  332.1 9.7 %copy-start.14 = (bf16[2,512,8,64]{1,3,2,0:T(8,128)(2,1)S(1)}, bf16[2,512,8,64]{1,3,2,0:T(8,128)(2,1)}, u32[]{:S(2)}) copy-start(bf16[2,512,8,64]{1,3,2,0:T(8,128)(2,1)} %get-tuple-element.711) | copy-start | bytes 3145732 | tf_op jit(solution)/shard_map/while
  356.6 11.5 %copy-start.8 = (f32[1024,8,64]{0,2,1:T(8,128)S(1)}, f32[1024,8,64]{0,2,1:T(8,128)}, u32[]{:S(2)}) copy-start(f32[1024,8,64]{0,2,1:T(8,128)} %get-tuple-element.693) | copy-start | bytes 6291460 | tf_op jit(solution)/shard_map/while
  356.6 11.5 %copy-start.13 = (bf16[2,512,8,64]{1,3,2,0:T(8,128)(2,1)S(1)}, bf16[2,512,8,64]{1,3,2,0:T(8,128)(2,1)}, u32[]{:S(2)}) copy-start(bf16[2,512,8,64]{1,3,2,0:T(8,128)(2,1)} %get-tuple-element.718) | copy-start | bytes 3145732 | tf_op jit(solution)/shard_map/while
  380.9 9.7 %copy-start.14 = (bf16[2,512,8,64]{1,3,2,0:T(8,128)(2,1)S(1)}, bf16[2,512,8,64]{1,3,2,0:T(8,128)(2,1)}, u32[]{:S(2)}) copy-start(bf16[2,512,8,64]{1,3,2,0:T(8,128)(2,1)} %get-tuple-element.711) | copy-start | bytes 3145732 | tf_op jit(solution)/shard_map/while
  405.5 11.5 %copy-start.8 = (f32[1024,8,64]{0,2,1:T(8,128)S(1)}, f32[1024,8,64]{0,2,1:T(8,128)}, u32[]{:S(2)}) copy-start(f32[1024,8,64]{0,2,1:T(8,128)} %get-tuple-element.693) | copy-start | bytes 6291460 | tf_op jit(solution)/shard_map/while
  405.5 11.5 %copy-start.13 = (bf16[2,512,8,64]{1,3,2,0:T(8,128)(2,1)S(1)}, bf16[2,512,8,64]{1,3,2,0:T(8,128)(2,1)}, u32[]{:S(2)}) copy-start(bf16[2,512,8,64]{1,3,2,0:T(8,128)(2,1)} %get-tuple-element.718) | copy-start | bytes 3145732 | tf_op jit(solution)/shard_map/while
  444.8 53.2 %all-to-all-start.3 = ((bf16[1024,3,512]{2,1,0:T(4,128)(2,1)}), bf16[1024,3,512]{2,1,0:T(4,128)(2,1)}, u32[]{:S(2)}, u32[]{:S(2)}) async-start(bf16[1024,3,512]{2,1,0:T(4,128)(2,1)} %copy.89), calls=%async_computation.3 | async-start | bytes 8388608 | tf_op jit(solution)/shard_map/all_to_all | solution.py:300
  450.6 231.4 %all-reduce.12.cloned.1.call-start = ((), (), s32[]{:S(2)}) async-start(), calls=%async_computation.8 | async-start | bytes 16777216 | tf_op jit(solution)/shard_map/psum | solution.py:308
  514.2 368.7 %all-reduce.14.cloned.1.call-start = ((), (), s32[]{:S(2)}) async-start(), calls=%async_computation.9 | async-start | bytes 16777216 | tf_op jit(solution)/shard_map/psum | solution.py:307
  682.7 8.6 copy-start.54
  (74 other events, 305.3 us)
Sparse Core Ops, SparseCore 0:
  10.3 64.6 all-gather.5
  77.2 40.2 all-gather.7
  119.6 73.0 all-gather.9
  194.7 72.9 all-gather.11
  514.3 167.6 all-reduce.11
  684.9 197.9 all-reduce.13
